TPU v7x, 32 devices: a whole 2x2x4 slice. The times are simulated.
32 devices in a mesh: dp: 4 (over y, core), tp: 8 (over z, x).
Axes of the slice: x: 2, y: 2, z: 4, core: 2. Of those that a mesh axis runs over, the one named last changes fastest.
Arguments:
- tokens: bfloat16 [1024, 7168], P(('dp', 'tp')), may hold values from -6 to 6
- w_gate: bfloat16 [7168, 12288], P(None, 'tp'), may hold values from -0.0625 to 0.0625
- w_up: bfloat16 [7168, 12288], P(None, 'tp'), may hold values from -0.0625 to 0.0625
- w_down: bfloat16 [12288, 7168], P('tp'), may hold values from -0.0546875 to 0.0546875
- cotangent: bfloat16 [1024, 7168], P(('dp', 'tp')), may hold values from -6 to 6
Outputs:
- mixed: bfloat16 [1024, 7168], P(('dp', 'tp'))
- input_grad: bfloat16 [1024, 7168], P(('dp', 'tp'))
- gate_grad: float32 [7168, 12288], P('dp', 'tp')
- up_grad: float32 [7168, 12288], P('dp', 'tp')
- down_grad: float32 [12288, 7168], P('tp', 'dp')
All inputs are finite; a program needn't handle non-finite values.
Results may differ from a plain program's by a relative error of at most 0.0049.
Values may be sent and summed in bfloat16 or wider, within the bound.
A program may use at most 192 MiB of HBM per device.

v0:
```python
import functools

import jax
import jax.numpy as jnp
from jax import lax
from jax.experimental import pallas as pl
from jax.experimental.pallas import tpu as pltpu
from jax.sharding import PartitionSpec as P


BF16 = jnp.bfloat16
F32 = jnp.float32


def right_trans(left, matrix):
    return lax.dot_general(left, matrix, (((1,), (1,)), ((), ())), preferred_element_type=F32)


def send_xor(block, bit, count):
    return lax.ppermute(block, "dp", [(i, i ^ bit) for i in range(count)])


def send_tp(block, dz, dx, count):
    ring = count // 2
    perm = [(i, ((i // 2 + dz) % ring) * 2 + ((i % 2) ^ dx)) for i in range(count)]
    return lax.ppermute(block, "tp", perm)


def gather_tp(own, count):
    if count != 8:
        whole = lax.all_gather(own, "tp", axis=0)
        return [whole[i] for i in range(count)]
    send = functools.partial(send_tp, count=count)
    across = send(own, 0, 1)
    below = send(own, 1, 0)
    above = send(own, -1, 0)
    across_above = send(above, 0, 1)
    across_below = send(across, 1, 0)
    far = send(above, -1, 0)
    half = own.shape[1] // 256 * 128
    left, right = across_above[:, :half], across_below[:, half:]
    left, right = send(left, -1, 0), send(right, 1, 0)
    across_far = jnp.concatenate([left, right], axis=1)
    return [own, across, above, across_above, far, across_far, below, across_below]


def scatter_tp(partial, count):
    rows = partial.shape[0] // count
    if count != 8:
        return lax.psum_scatter(partial.astype(F32), "tp", scatter_dimension=0, tiled=True).astype(BF16)
    send = functools.partial(send_tp, count=count)
    half = partial.shape[1] // 256 * 128
    near, above, far, below = (partial[i * 2 * rows : (i + 1) * 2 * rows] for i in range(4))
    left, right = far[:, :half], far[:, half:]
    from_below, from_above = send(left, 1, 0), send(right, -1, 0)
    up = jnp.concatenate(
        [(above[:, :half].astype(F32) + from_below.astype(F32)).astype(BF16), above[:, half:]], axis=1
    )
    down = jnp.concatenate(
        [below[:, :half], (below[:, half:].astype(F32) + from_above.astype(F32)).astype(BF16)], axis=1
    )
    up, down = send(up, 1, 0), send(down, -1, 0)
    total = near.astype(F32) + up.astype(F32) + down.astype(F32)
    crossed = total[rows:].astype(BF16)
    crossed = send(crossed, 0, 1)
    return (total[:rows] + crossed.astype(F32)).astype(BF16)


def gather_dp(own, count):
    blocks = {0: own}
    bit = count // 2
    while bit:
        blocks.update({k | bit: send_xor(b, bit, count) for k, b in list(blocks.items())})
        bit //= 2
    return [blocks[k] for k in range(count)]


def grad_kernel(count, *refs):
    lefts, rights, out = refs[:count], refs[count : 2 * count], refs[-1]
    total = None
    for left, right in zip(lefts, rights):
        part = lax.dot_general(
            left[...], right[...], (((0,), (0,)), ((), ())), preferred_element_type=F32
        )
        total = part if total is None else total + part
    out[...] = total


def token_sum(lefts, rights):
    count = len(lefts)
    tokens, rows = lefts[0].shape
    cols = rights[0].shape[1]
    tile = 256 if rows % 256 == 0 else 128
    return pl.pallas_call(
        functools.partial(grad_kernel, count),
        grid=(rows // tile,),
        in_specs=[pl.BlockSpec((tokens, tile), lambda i: (0, i))] * count
        + [pl.BlockSpec((tokens, cols), lambda i: (0, 0))] * count,
        out_specs=pl.BlockSpec((tile, cols), lambda i: (i, 0)),
        out_shape=jax.ShapeDtypeStruct((rows, cols), F32),
        cost_estimate=pl.CostEstimate(
            flops=2 * count * tokens * rows * cols,
            bytes_accessed=2 * count * tokens * (rows + cols) + 4 * rows * cols,
            transcendentals=0,
        ),
        compiler_params=pltpu.CompilerParams(vmem_limit_bytes=32 << 20),
    )(*lefts, *rights)


def body(dp, tp, tokens, w_gate, w_up, w_down, cotangent):
    me = lax.axis_index("dp")
    part = tokens.shape[1] // dp

    def features(x, k):
        return lax.dynamic_slice_in_dim(x, (me ^ k) * part, part, axis=1)

    gathered = jnp.concatenate(gather_tp(tokens, tp), axis=0)
    gate = jnp.dot(gathered, w_gate, preferred_element_type=F32)
    up = jnp.dot(gathered, w_up, preferred_element_type=F32)

    grads = gather_tp(cotangent, tp)
    grad_full = jnp.concatenate(grads, axis=0)

    sig = jax.nn.sigmoid(gate)
    act = gate * sig
    hidden = (act * up).astype(BF16)
    gate, up, hidden = lax.optimization_barrier((gate, up, hidden))
    mixed = jnp.dot(hidden, w_down, preferred_element_type=F32).astype(BF16)
    sig = jax.nn.sigmoid(gate)
    act = gate * sig
    back = right_trans(grad_full, w_down)
    dgate = (back * up * sig * (1.0 + gate * (1.0 - sig))).astype(BF16)
    dup = (back * act).astype(BF16)

    mixed = scatter_tp(mixed, tp)
    partial = (right_trans(dgate, w_gate) + right_trans(dup, w_up)).astype(BF16)
    input_grad = scatter_tp(partial, tp)

    token_parts = [features(gathered, 0)] + [
        send_xor(features(gathered, k), k, dp) for k in range(1, dp)
    ]

    far = [send_xor(features(cotangent, k), k, dp) for k in range(2, dp)]
    rows = cotangent.shape[0]
    far = gather_tp(jnp.concatenate(far, axis=0), tp)
    grad_parts = [features(grad_full, 0), send_xor(features(grad_full, 1), 1, dp)] + [
        jnp.concatenate([f[i * rows : (i + 1) * rows] for f in far], axis=0) for i in range(dp - 2)
    ]

    all_hidden = gather_dp(hidden, dp)
    all_dgate = gather_dp(dgate, dp)
    all_dup = gather_dp(dup, dp)
    down_grad = token_sum(all_hidden, grad_parts)
    gate_grad = token_sum(token_parts, all_dgate)
    up_grad = token_sum(token_parts, all_dup)
    return (mixed, input_grad, gate_grad, up_grad, down_grad)


MESH = pl.DeviceIdType.MESH
CORES, COLS = 2, 2


def fused_kernel(
    tokens, cotangent, w_gate, w_up, w_down,
    mixed, input_grad, features, units,
    blocks, gate, up, back, hidden, dgate, dup, partial, from_x, from_below, from_above, onward,
    gu_tiles, down_tiles, in_tiles,
    own_sem, gu_sem, down_sem, in_sem,
    up_send, up_recv, dn_send, dn_recv, x_send, x_recv,
    ex_send, ex_recv, un_send, un_recv, un_local,
    rx_send, rx_recv, rz_send, ru_recv, rd_recv,
):
    me, place = lax.axis_index("dp"), lax.axis_index("tp")
    z, x = place // COLS, place % COLS
    y, core = me // CORES, me % CORES
    rows, _ = tokens.shape
    steps, held, part = blocks.shape[0] // 2, blocks.shape[1], blocks.shape[2]
    levels = held // rows // COLS
    column = levels * rows
    inner = gate.shape[1]
    half, slab = inner // 2, part // 2
    top = levels - 1
    beside = (me, z * COLS + (1 - x))
    above, below = (me, place + COLS), (me, place - COLS)
    twin = y * CORES + (1 - core)
    across = (1 - y) * CORES + core

    def chunk(g):
        s = lax.rem(g, steps)
        return lax.rem(s + 1 + y, 2) * 2 + s // 2

    def remote(src, dst, send, recv, device):
        return pltpu.make_async_remote_copy(
            src_ref=src, dst_ref=dst, send_sem=send, recv_sem=recv, device_id=device, device_id_type=MESH
        )

    def spot(g, col, level):
        return blocks.at[g, pl.ds(pl.multiple_of((col * levels + level) * rows, rows), rows), :]

    def go_up(g, h):
        ref = spot(g, x, z - h)
        return remote(ref, ref, up_send.at[g, h], up_recv.at[g, h], above)

    def go_down(g, h):
        ref = spot(g, x, z + h)
        return remote(ref, ref, dn_send.at[g, h], dn_recv.at[g, h], below)

    def go_x(g, level):
        ref = spot(g, x, level)
        return remote(ref, ref, x_send.at[g, level], x_recv.at[g, level], beside)

    def own(g):
        @pl.when(z < top)
        def _():
            go_up(g, 0).start()

        @pl.when(z > 0)
        def _():
            go_down(g, 0).start()

        go_x(g, z).start()

    def relay(g, h):
        @pl.when(z >= h)
        def _():
            ref = spot(g, x, z - h)
            remote(ref, ref, up_send.at[g, h - 1], up_recv.at[g, h - 1], below).wait_recv()
            if h < top:
                @pl.when(z < top)
                def _():
                    go_up(g, h).start()

            go_x(g, z - h).start()

        @pl.when(z + h <= top)
        def _():
            ref = spot(g, x, z + h)
            remote(ref, ref, dn_send.at[g, h - 1], dn_recv.at[g, h - 1], above).wait_recv()
            if h < top:
                @pl.when(z > 0)
                def _():
                    go_down(g, h).start()

            go_x(g, z + h).start()

    def arrived(g):
        for level in range(levels):
            ref = spot(g, 1 - x, level)
            remote(ref, ref, x_send.at[g, level], x_recv.at[g, level], beside).wait_recv()

    def exchange(g):
        to, kind = chunk(g), g // steps

        @pl.when(to == me)
        def _():
            pltpu.make_async_copy(blocks.at[g], features.at[kind, me], ex_send.at[g]).start()

        @pl.when(to != me)
        def _():
            remote(
                blocks.at[g], features.at[kind, me], ex_send.at[g], ex_recv.at[kind, me], (to, place)
            ).start()

    def exchange_done(g):
        to, kind = chunk(g), g // steps

        @pl.when(to == me)
        def _():
            pltpu.make_async_copy(blocks.at[g], features.at[kind, me], ex_send.at[g]).wait()

        @pl.when(to != me)
        def _():
            remote(
                blocks.at[g], features.at[kind, me], ex_send.at[g], ex_recv.at[kind, me], (to, place)
            ).wait_send()

    def units_copies(src, k):
        dst = units.at[k, me]
        return (
            pltpu.make_async_copy(src, dst, un_local.at[k]),
            remote(src, dst, un_send.at[k, 0], un_recv.at[k, me], (across, place)),
            remote(src, dst, un_send.at[k, 1], un_recv.at[k, me], (twin, place)),
        )

    def units_forward(k):
        ref = units.at[k, across]
        return remote(ref, ref, un_send.at[k, 2], un_recv.at[k, across], (twin, place))

    def units_arrived(k, who):
        ref = units.at[k, who]
        remote(ref, ref, un_send.at[k, 2], un_recv.at[k, who], (twin, place)).wait_recv()

    def gu_copy(g, t):
        source = w_gate if t < 2 else w_up
        return pltpu.make_async_copy(
            source.at[pl.ds(pl.multiple_of(chunk(g) * part, 128), part), (t % 2) * half : (t % 2 + 1) * half],
            gu_tiles.at[t % 2],
            gu_sem.at[t % 2],
        )

    def down_copy(g, t):
        return pltpu.make_async_copy(
            w_down.at[t * half : (t + 1) * half, pl.ds(pl.multiple_of(chunk(g) * part, 128), part)],
            down_tiles.at[t],
            down_sem.at[t],
        )

    def in_copy(j, t, k):
        start = chunk(j) * part + t * slab
        return pltpu.make_async_copy(
            (w_gate, w_up)[k].at[pl.ds(pl.multiple_of(start, 128), slab), :],
            in_tiles.at[t, k],
            in_sem.at[t, k],
        )

    def rs_x(q):
        src = partial.at[q, pl.ds(pl.multiple_of((1 - x) * column, rows), column), :]
        return remote(src, from_x.at[q], rx_send.at[q], rx_recv.at[q], beside)

    def rs_up(q, first, count):
        return remote(
            onward.at[q, first * rows : (first + count) * rows, :],
            from_below.at[q, 0 : count * rows, :],
            rz_send.at[q, 0], ru_recv.at[q], above,
        )

    def rs_down(q, first, count):
        return remote(
            onward.at[q, first * rows : (first + count) * rows, :],
            from_above.at[q, 0 : count * rows, :],
            rz_send.at[q, 1], rd_recv.at[q], below,
        )

    def below_arrived(q, count):
        ref = from_below.at[q, 0 : count * rows, :]
        remote(ref, ref, rz_send.at[q, 0], ru_recv.at[q], below).wait_recv()

    def above_arrived(q, count):
        ref = from_above.at[q, 0 : count * rows, :]
        remote(ref, ref, rz_send.at[q, 1], rd_recv.at[q], above).wait_recv()

    def total(q, level, *more):
        mine = partial[q, pl.ds(pl.multiple_of(x * column + level * rows, rows), rows), :].astype(F32)
        mine += from_x[q, level * rows : (level + 1) * rows, :].astype(F32)
        for ref, at in more:
            mine += ref[q, at * rows : (at + 1) * rows, :].astype(F32)
        return mine.astype(BF16)

    def put(q, at, value):
        onward[q, at * rows : (at + 1) * rows, :] = value

    def emit(q, value):
        cols = pl.ds(pl.multiple_of(chunk(q) * part, 128), part)

        @pl.when(q < steps)
        def _():
            mixed[:, cols] = value

        @pl.when(q >= steps)
        def _():
            input_grad[:, cols] = value

    def stage_one(q):
        rs_x(q).wait_recv()

        @pl.when(z == 0)
        def _():
            for level in (1, 2, 3):
                put(q, level - 1, total(q, level))
            rs_up(q, 0, 3).start()

        @pl.when(z == 3)
        def _():
            for level in (0, 1, 2):
                put(q, level, total(q, level))
            rs_down(q, 0, 3).start()

    def stage_two(q):
        @pl.when(z == 1)
        def _():
            below_arrived(q, 3)
            for level in (2, 3):
                put(q, level - 2, total(q, level, (from_below, level - 1)))
            rs_up(q, 0, 2).start()

        @pl.when(z == 2)
        def _():
            above_arrived(q, 3)
            for level in (0, 1):
                put(q, level, total(q, level, (from_above, level)))
            rs_down(q, 0, 2).start()

    def stage_three(q):
        @pl.when(z == 2)
        def _():
            below_arrived(q, 2)
            put(q, 2, total(q, 3, (from_below, 1)))
            rs_up(q, 2, 1).start()

        @pl.when(z == 1)
        def _():
            above_arrived(q, 2)
            put(q, 2, total(q, 0, (from_above, 0)))
            rs_down(q, 2, 1).start()

    def stage_four(q):
        @pl.when(z == 0)
        def _():
            above_arrived(q, 1)
            emit(q, total(q, 0, (from_above, 0)))

        @pl.when(z == 1)
        def _():
            emit(q, total(q, 1, (from_below, 0), (from_above, 1)))

        @pl.when(z == 2)
        def _():
            emit(q, total(q, 2, (from_below, 0), (from_above, 2)))

        @pl.when(z == 3)
        def _():
            below_arrived(q, 1)
            emit(q, total(q, 3, (from_below, 0)))

    mine = pl.ds(pl.multiple_of((x * levels + z) * rows, rows), rows)

    def own_copy(g, source):
        return pltpu.make_async_copy(
            source.at[:, pl.ds(pl.multiple_of(chunk(g) * part, 128), part)], blocks.at[g, mine, :], own_sem.at[g]
        )

    for s in range(steps):
        own_copy(s, tokens).start()
    for s in range(steps):
        own_copy(steps + s, cotangent).start()
    for t in range(2):
        gu_copy(0, t).start()
        down_copy(steps, t).start()
        for k in range(2):
            in_copy(0, t, k).start()

    barrier = pltpu.get_barrier_semaphore()

    def greet(device):
        pl.semaphore_signal(barrier, inc=1, device_id=device, device_id_type=MESH)

    greet(beside)
    for other in (twin, across, (1 - y) * CORES + (1 - core)):
        greet((other, place))

    @pl.when(z < top)
    def _():
        greet(above)

    @pl.when(z > 0)
    def _():
        greet(below)

    @pl.when((z > 0) & (z < top))
    def _():
        pl.semaphore_wait(barrier, 6)

    @pl.when((z == 0) | (z == top))
    def _():
        pl.semaphore_wait(barrier, 5)

    for s in range(steps):
        own_copy(s, tokens).wait()
        own_copy(steps + s, cotangent).wait()

    own(0)
    own(1)
    gate[...] = jnp.zeros_like(gate)
    up[...] = jnp.zeros_like(up)
    back[...] = jnp.zeros_like(back)
    for h in range(1, levels):
        relay(0, h)

    @pl.loop(0, steps)
    def _(g):
        own(g + 2)
        relay(g + 1, 1)
        arrived(g)
        exchange(g)
        for t in range(4):
            gu_copy(g, t).wait()
            target, at = (gate, up)[t // 2], t % 2
            target[:, at * half : (at + 1) * half] += jnp.dot(
                blocks[g], gu_tiles[at], preferred_element_type=F32
            )
            if t < 2:
                gu_copy(g, t + 2).start()
            else:
                @pl.when(g < steps - 1)
                def _():
                    gu_copy(g + 1, t - 2).start()
            if t in (1, 3):
                relay(g + 1, t // 2 + 2)

    lines = 32

    @pl.loop(0, held // lines)
    def _(i):
        at = pl.ds(pl.multiple_of(i * lines, lines), lines)
        value = gate[at, :]
        hidden[at, :] = (value * jax.nn.sigmoid(value) * up[at, :]).astype(BF16)

    for copy in units_copies(hidden, 0):
        copy.start()

    @pl.loop(steps, 2 * steps)
    def _(g):
        @pl.when(g + 2 < 2 * steps)
        def _():
            own(g + 2)

        @pl.when(g + 1 < 2 * steps)
        def _():
            relay(g + 1, 1)

        for t in range(2):
            down_copy(g, t).wait()
        product = jnp.dot(hidden[:, :half], down_tiles[0], preferred_element_type=F32)
        product += jnp.dot(hidden[:, half:], down_tiles[1], preferred_element_type=F32)
        partial[g - steps] = product.astype(BF16)

        @pl.when(g + 1 < 2 * steps)
        def _():
            relay(g + 1, 2)

        arrived(g)
        exchange(g)
        for t in range(2):
            back[:, t * half : (t + 1) * half] += right_trans(blocks[g], down_tiles[t])

            @pl.when(g + 1 < 2 * steps)
            def _():
                down_copy(g + 1, t).start()

        @pl.when(g + 1 < 2 * steps)
        def _():
            relay(g + 1, 3)

        @pl.when(g == 2 * steps - 2)
        def _():
            for j in range(steps - 1):
                rs_x(j).start()

    rs_x(steps - 1).start()

    @pl.loop(0, held // lines)
    def _(i):
        at = pl.ds(pl.multiple_of(i * lines, lines), lines)
        value, other, grad = gate[at, :], up[at, :], back[at, :]
        sig = jax.nn.sigmoid(value)
        dgate[at, :] = (grad * other * sig * (1.0 + value * (1.0 - sig))).astype(BF16)
        dup[at, :] = (grad * (value * sig)).astype(BF16)

    for k, source in ((1, dgate), (2, dup)):
        for copy in units_copies(source, k):
            copy.start()
    units_arrived(0, across)
    units_forward(0).start()

    last = 2 * steps

    @pl.loop(0, last + 3)
    def _(i):
        @pl.when(i < steps)
        def _():
            for t in range(2):
                for k in range(2):
                    in_copy(i, t, k).wait()
                product = right_trans(dgate[...], in_tiles[t, 0]) + right_trans(dup[...], in_tiles[t, 1])
                partial[i + steps, :, t * slab : (t + 1) * slab] = product.astype(BF16)

                @pl.when(i + 1 < steps)
                def _():
                    for k in range(2):
                        in_copy(i + 1, t, k).start()
            rs_x(i + steps).start()

        @pl.when(i < last)
        def _():
            stage_one(i)

        @pl.when((i >= 1) & (i < last + 1))
        def _():
            stage_two(i - 1)

        @pl.when((i >= 2) & (i < last + 2))
        def _():
            stage_three(i - 2)

        @pl.when(i >= 3)
        def _():
            stage_four(i - 3)

        @pl.when(i == last)
        def _():
            units_arrived(1, across)
            units_forward(1).start()

    units_arrived(2, across)
    units_forward(2).start()

    @pl.loop(0, 2 * steps)
    def _(g):
        for h in range(top):
            @pl.when((z < top) & (z >= h))
            def _():
                go_up(g, h).wait_send()

            @pl.when((z > 0) & (z + h <= top))
            def _():
                go_down(g, h).wait_send()

        for level in range(levels):
            go_x(g, level).wait_send()
        exchange_done(g)
        rs_x(g).wait_send()

        @pl.when(z == 0)
        def _():
            rs_up(g, 0, 3).wait_send()

        @pl.when(z == 1)
        def _():
            rs_up(g, 0, 2).wait_send()
            rs_down(g, 2, 1).wait_send()

        @pl.when(z == 2)
        def _():
            rs_up(g, 2, 1).wait_send()
            rs_down(g, 0, 2).wait_send()

        @pl.when(z == 3)
        def _():
            rs_down(g, 0, 3).wait_send()

    for kind in range(2):
        for other in (twin, across, (1 - y) * CORES + (1 - core)):
            ref = features.at[kind, other]
            remote(ref, ref, ex_send.at[0], ex_recv.at[kind, other], (twin, place)).wait_recv()
    for k, source in enumerate((hidden, dgate, dup)):
        local, far, near = units_copies(source, k)
        local.wait()
        far.wait_send()
        near.wait_send()
        units_forward(k).wait_send()
        units_arrived(k, twin)
        units_arrived(k, (1 - y) * CORES + (1 - core))


def fused_body(dp, tp, tokens, w_gate, w_up, w_down, cotangent):
    rows, width = tokens.shape
    inner = w_gate.shape[1]
    held, part = rows * tp, width // dp
    levels = tp // COLS
    half, slab = inner // 2, part // 2
    hbm, vmem = pl.BlockSpec(memory_space=pl.ANY), pl.BlockSpec(memory_space=pltpu.VMEM)
    dma = pltpu.SemaphoreType.DMA
    chain = (levels - 1) * rows
    mixed, input_grad, features, units = pl.pallas_call(
        fused_kernel,
        in_specs=[hbm] * 5,
        out_specs=[vmem, vmem, hbm, hbm],
        out_shape=[
            jax.ShapeDtypeStruct((rows, width), BF16),
            jax.ShapeDtypeStruct((rows, width), BF16),
            jax.ShapeDtypeStruct((2, dp, held, part), BF16),
            jax.ShapeDtypeStruct((3, dp, held, inner), BF16),
        ],
        scratch_shapes=[
            pltpu.VMEM((2 * dp, held, part), BF16),
            pltpu.VMEM((held, inner), F32),
            pltpu.VMEM((held, inner), F32),
            pltpu.VMEM((held, inner), F32),
            pltpu.VMEM((held, inner), BF16),
            pltpu.VMEM((held, inner), BF16),
            pltpu.VMEM((held, inner), BF16),
            pltpu.VMEM((2 * dp, held, part), BF16),
            pltpu.VMEM((2 * dp, levels * rows, part), BF16),
            pltpu.VMEM((2 * dp, chain, part), BF16),
            pltpu.VMEM((2 * dp, chain, part), BF16),
            pltpu.VMEM((2 * dp, chain, part), BF16),
            pltpu.VMEM((2, part, half), BF16),
            pltpu.VMEM((2, half, part), BF16),
            pltpu.VMEM((2, 2, slab, inner), BF16),
            dma((2 * dp,)), dma((2,)), dma((2,)), dma((2, 2)),
            dma((2 * dp, 3)), dma((2 * dp, 3)), dma((2 * dp, 3)), dma((2 * dp, 3)),
            dma((2 * dp, levels)), dma((2 * dp, levels)),
            dma((2 * dp,)), dma((2, dp)),
            dma((3, 3)), dma((3, dp)), dma((3,)),
            dma((2 * dp,)), dma((2 * dp,)), dma((2 * dp, 2)), dma((2 * dp,)), dma((2 * dp,)),
        ],
        compiler_params=pltpu.CompilerParams(
            collective_id=0, has_side_effects=True, vmem_limit_bytes=67_043_328
        ),
        name="fused",
    )(tokens, cotangent, w_gate, w_up, w_down)

    def grad(left, at, right, of):
        count = left.shape[-1]
        cols = right.shape[-1]
        tile = count // 2 if count % 256 == 0 else 128

        def kernel(l_ref, r_ref, out):
            out[...] = lax.dot_general(
                l_ref[...].reshape(dp * held, tile),
                r_ref[...].reshape(dp * held, cols),
                (((0,), (0,)), ((), ())),
                preferred_element_type=F32,
            )

        return pl.pallas_call(
            kernel,
            grid=(count // tile,),
            in_specs=[
                pl.BlockSpec((None, dp, held, tile), lambda i: (at, 0, 0, i)),
                pl.BlockSpec((None, dp, held, cols), lambda i: (of, 0, 0, 0)),
            ],
            out_specs=pl.BlockSpec((tile, cols), lambda i: (i, 0)),
            out_shape=jax.ShapeDtypeStruct((count, cols), F32),
            compiler_params=pltpu.CompilerParams(vmem_limit_bytes=60 << 20),
        )(left, right)

    gate_grad = grad(features, 0, units, 1)
    up_grad = grad(features, 0, units, 2)
    down_grad = grad(units, 0, features, 1)
    return mixed, input_grad, gate_grad, up_grad, down_grad


def solution(mesh):
    in_specs = (
        P(("dp", "tp"), None),
        P(None, "tp"),
        P(None, "tp"),
        P("tp", None),
        P(("dp", "tp"), None),
    )
    out_specs = (
        P(("dp", "tp"), None),
        P(("dp", "tp"), None),
        P("dp", "tp"),
        P("dp", "tp"),
        P("tp", "dp"),
    )

    def run(*args):
        chosen = fused_body if (mesh.shape["dp"], mesh.shape["tp"]) == (4, 8) else body
        return chosen(mesh.shape["dp"], mesh.shape["tp"], *args)

    return jax.shard_map(run, mesh=mesh, in_specs=in_specs, out_specs=out_specs, check_vma=False)
```

profile of v0, /device:TPU:0, one launch (start us, length us, event | category | flops | bytes accessed | tf_op | source)
XLA Modules:
  0.0 225.6 jit_solution(10416975280684771738)
XLA Ops:
  0.6 190.3 %fused.1 = (bf16[32,7168]{1,0:T(8,128)(2,1)}, bf16[32,7168]{1,0:T(8,128)(2,1)}, bf16[2,4,256,1792]{3,2,1,0:T(8,128)(2,1)}, bf16[3,4,256,1536]{3,2,1,0:T(8,128)(2,1)}) custom-call(bf16[32,7168]{1,0:T(8,128)(2,1)} %tokens.1, bf16[32,7168]{1,0:T(8,128)(2,1)} %cotangent.1, bf16[7168,1536]{1,0:T(8,128)(2,1)} %w_gate.1, bf16[7168,1536]{1,0:T(8,128)(2,1)} %w_up.1, ...), custom_call_target="tpu_custom_call" | custom-call | tf_op jit(solution)/shard_map/fused/pallas_call | solution.py:664
  190.9 11.1 %shard_map.94 = f32[1536,1792]{1,0:T(8,128)} custom-call(bf16[3,4,256,1536]{3,2,1,0:T(8,128)(2,1)} %get-tuple-element.12.r_ref.l_ref, bf16[2,4,256,1792]{3,2,1,0:T(8,128)(2,1)} %get-tuple-element.11.l_ref.r_ref), custom_call_target="tpu_custom_call" | custom-call | tf_op jit(solution)/shard_map/pallas_call | solution.py:716
  202.0 11.0 %shard_map.93 = f32[1792,1536]{1,0:T(8,128)} custom-call(bf16[2,4,256,1792]{3,2,1,0:T(8,128)(2,1)} %get-tuple-element.11.l_ref.r_ref, bf16[3,4,256,1536]{3,2,1,0:T(8,128)(2,1)} %get-tuple-element.12.r_ref.l_ref), custom_call_target="tpu_custom_call" | custom-call | tf_op jit(solution)/shard_map/pallas_call | solution.py:716
  213.0 0.0 copy-start.1
  213.0 0.0 copy-start
  213.0 11.1 %shard_map.92 = f32[1792,1536]{1,0:T(8,128)} custom-call(bf16[2,4,256,1792]{3,2,1,0:T(8,128)(2,1)} %get-tuple-element.11.l_ref.r_ref, bf16[3,4,256,1536]{3,2,1,0:T(8,128)(2,1)} %get-tuple-element.12.r_ref.l_ref), custom_call_target="tpu_custom_call" | custom-call | tf_op jit(solution)/shard_map/pallas_call | solution.py:716
  224.1 0.0 copy-done.1
  224.1 0.8 copy.12
  224.8 0.0 copy-done
  224.8 0.8 copy.13
Async XLA Ops:
  213.0 11.1 %copy-start.1 = (bf16[32,7168]{1,0:T(8,128)(2,1)S(1)}, bf16[32,7168]{1,0:T(8,128)(2,1)}, u32[]{:S(2)}) copy-start(bf16[32,7168]{1,0:T(8,128)(2,1)} %get-tuple-element.18) | copy-start | bytes 1376260
  213.0 11.8 %copy-start = (bf16[32,7168]{1,0:T(8,128)(2,1)S(1)}, bf16[32,7168]{1,0:T(8,128)(2,1)}, u32[]{:S(2)}) copy-start(bf16[32,7168]{1,0:T(8,128)(2,1)} %get-tuple-element.19) | copy-start | bytes 1376260
where the time goes:
time: 226 us
  Pallas kernels  223 us (99%)
    pallas_call x1, Pallas kernels, fused_body(): pl.pallas_call(fused_kernel, in_specs=[hbm] * 5, out_specs=[vmem, vmem, h...  190 us
    pallas_call x3, Pallas kernels, grad(): pl.pallas_call(kernel, grid=(count // tile,), in_specs=[pl.BlockSpec((Non...  33.1 us

commit v1 on v0

--- a/solution.py
+++ b/solution.py
@@ -157,16 +157,18 @@
 
 
 MESH = pl.DeviceIdType.MESH
-CORES, COLS = 2, 2
+CORES, COLS, HALVES = 2, 2, 2
 
 
 def fused_kernel(
     tokens, cotangent, w_gate, w_up, w_down,
     mixed, input_grad, features, units,
     blocks, gate, up, back, hidden, dgate, dup, partial, from_x, from_below, from_above, onward,
+    edge_out, edge_in, edge_keep,
     gu_tiles, down_tiles, in_tiles,
     own_sem, gu_sem, down_sem, in_sem,
     up_send, up_recv, dn_send, dn_recv, x_send, x_recv,
+    eu_send, eu_recv, ed_send, ed_recv, ee_send, ee_recv,
     ex_send, ex_recv, un_send, un_recv, un_local,
     rx_send, rx_recv, rz_send, ru_recv, rd_recv,
 ):
@@ -178,24 +180,34 @@
     levels = held // rows // COLS
     column = levels * rows
     inner = gate.shape[1]
-    half, slab = inner // 2, part // 2
+    half = inner // 2
+    edge = part // 7 // 128 * 128
+    main = part - edge
+    ahead = 8
     top = levels - 1
     beside = (me, z * COLS + (1 - x))
     above, below = (me, place + COLS), (me, place - COLS)
     twin = y * CORES + (1 - core)
     across = (1 - y) * CORES + core
 
-    def chunk(g):
-        s = lax.rem(g, steps)
+    def owner(g):
+        s = lax.rem(g, steps) // HALVES
         return lax.rem(s + 1 + y, 2) * 2 + s // 2
+
+    def at_column(g):
+        return pl.multiple_of((owner(g) * HALVES + lax.rem(g, HALVES)) * part, 128)
 
     def remote(src, dst, send, recv, device):
         return pltpu.make_async_remote_copy(
             src_ref=src, dst_ref=dst, send_sem=send, recv_sem=recv, device_id=device, device_id_type=MESH
         )
 
-    def spot(g, col, level):
-        return blocks.at[g, pl.ds(pl.multiple_of((col * levels + level) * rows, rows), rows), :]
+    def spot(g, col, level, first=0, last=None):
+        last = part if last is None else last
+        return blocks.at[g, pl.ds(pl.multiple_of((col * levels + level) * rows, rows), rows), first:last]
+
+    def rim(g, col, level):
+        return spot(g, col, level, main, part)
 
     def go_up(g, h):
         ref = spot(g, x, z - h)
@@ -205,11 +217,31 @@
         ref = spot(g, x, z + h)
         return remote(ref, ref, dn_send.at[g, h], dn_recv.at[g, h], below)
 
+    def rim_up(g, h):
+        ref = rim(g, 1 - x, z - h)
+        return remote(ref, ref, eu_send.at[g, h], eu_recv.at[g, h], above)
+
+    def rim_down(g, h):
+        ref = rim(g, 1 - x, z + h)
+        return remote(ref, ref, ed_send.at[g, h], ed_recv.at[g, h], below)
+
+    def own_x(g):
+        ref = spot(g, x, z)
+        return remote(ref, ref, x_send.at[g, z], x_recv.at[g, z], beside)
+
     def go_x(g, level):
-        ref = spot(g, x, level)
+        ref = spot(g, x, level, 0, main)
         return remote(ref, ref, x_send.at[g, level], x_recv.at[g, level], beside)
 
     def own(g):
+        @pl.when(g < steps)
+        def _():
+            own_copy(g, tokens).wait()
+
+        @pl.when(g >= steps)
+        def _():
+            own_copy(g, cotangent).wait()
+
         @pl.when(z < top)
         def _():
             go_up(g, 0).start()
@@ -218,7 +250,20 @@
         def _():
             go_down(g, 0).start()
 
-        go_x(g, z).start()
+        own_x(g).start()
+        share(g, z)
+
+    def turn(g):
+        ref = spot(g, 1 - x, z)
+        remote(ref, ref, x_send.at[g, z], x_recv.at[g, z], beside).wait_recv()
+
+        @pl.when(z < top)
+        def _():
+            rim_up(g, 0).start()
+
+        @pl.when(z > 0)
+        def _():
+            rim_down(g, 0).start()
 
     def relay(g, h):
         @pl.when(z >= h)
@@ -231,6 +276,7 @@
                     go_up(g, h).start()
 
             go_x(g, z - h).start()
+            share(g, z - h)
 
         @pl.when(z + h <= top)
         def _():
@@ -242,37 +288,102 @@
                     go_down(g, h).start()
 
             go_x(g, z + h).start()
+            share(g, z + h)
+
+    def relay_rim(g, h):
+        @pl.when(z >= h)
+        def _():
+            ref = rim(g, 1 - x, z - h)
+            remote(ref, ref, eu_send.at[g, h - 1], eu_recv.at[g, h - 1], below).wait_recv()
+            if h < top:
+                @pl.when(z < top)
+                def _():
+                    rim_up(g, h).start()
+
+        @pl.when(z + h <= top)
+        def _():
+            ref = rim(g, 1 - x, z + h)
+            remote(ref, ref, ed_send.at[g, h - 1], ed_recv.at[g, h - 1], above).wait_recv()
+            if h < top:
+                @pl.when(z > 0)
+                def _():
+                    rim_down(g, h).start()
+
+    def step_in(g, lag, act):
+        @pl.when((g + lag >= 0) & (g + lag < 2 * steps))
+        def _():
+            act(g + lag)
+
+    def first_acts(g):
+        step_in(g, ahead, own)
+        step_in(g, ahead - 2, turn)
+        step_in(g, ahead - 2, lambda c: relay(c, 1))
+        step_in(g, ahead - 4, lambda c: relay_rim(c, 1))
+
+    def second_acts(g):
+        step_in(g, ahead - 4, lambda c: relay(c, 2))
+        step_in(g, ahead - 6, lambda c: relay_rim(c, 2))
+
+    def third_acts(g):
+        step_in(g, ahead - 6, lambda c: relay(c, 3))
 
     def arrived(g):
-        for level in range(levels):
-            ref = spot(g, 1 - x, level)
-            remote(ref, ref, x_send.at[g, level], x_recv.at[g, level], beside).wait_recv()
+        relay_rim(g, 3)
+        for h in range(1, levels):
+            @pl.when(z >= h)
+            def _():
+                ref = spot(g, 1 - x, z - h, 0, main)
+                remote(ref, ref, x_send.at[g, z - h], x_recv.at[g, z - h], beside).wait_recv()
+
+            @pl.when(z + h <= top)
+            def _():
+                ref = spot(g, 1 - x, z + h, 0, main)
+                remote(ref, ref, x_send.at[g, z + h], x_recv.at[g, z + h], beside).wait_recv()
+
+    def shared(g, who):
+        piece = lax.rem(g, HALVES)
+        return features.at[g // steps, who, :, pl.ds(pl.multiple_of(piece * part, 128), part)]
+
+    def local_share(g):
+        return pltpu.make_async_copy(blocks.at[g], shared(g, me), ex_send.at[g, 0])
+
+    def lines_share(g, first, count, index):
+        lines = pl.ds(pl.multiple_of(first, rows), count)
+        recv = ex_recv.at[g // steps, me, lax.rem(g, HALVES), index]
+        return remote(
+            blocks.at[g, lines, :], shared(g, me).at[lines, :], ex_send.at[g, index], recv, (owner(g), place)
+        )
+
+    def block_share(g, level):
+        return lines_share(g, (x * levels + level) * rows, rows, level)
+
+    def rest_share(g):
+        return lines_share(g, (1 - x) * column, column, levels)
+
+    def share(g, level):
+        @pl.when(owner(g) != me)
+        def _():
+            block_share(g, level).start()
 
     def exchange(g):
-        to, kind = chunk(g), g // steps
-
-        @pl.when(to == me)
-        def _():
-            pltpu.make_async_copy(blocks.at[g], features.at[kind, me], ex_send.at[g]).start()
-
-        @pl.when(to != me)
-        def _():
-            remote(
-                blocks.at[g], features.at[kind, me], ex_send.at[g], ex_recv.at[kind, me], (to, place)
-            ).start()
+        @pl.when(owner(g) == me)
+        def _():
+            local_share(g).start()
+
+        @pl.when(owner(g) != me)
+        def _():
+            rest_share(g).start()
 
     def exchange_done(g):
-        to, kind = chunk(g), g // steps
-
-        @pl.when(to == me)
-        def _():
-            pltpu.make_async_copy(blocks.at[g], features.at[kind, me], ex_send.at[g]).wait()
-
-        @pl.when(to != me)
-        def _():
-            remote(
-                blocks.at[g], features.at[kind, me], ex_send.at[g], ex_recv.at[kind, me], (to, place)
-            ).wait_send()
+        @pl.when(owner(g) == me)
+        def _():
+            local_share(g).wait()
+
+        @pl.when(owner(g) != me)
+        def _():
+            for level in range(levels):
+                block_share(g, level).wait_send()
+            rest_share(g).wait_send()
 
     def units_copies(src, k):
         dst = units.at[k, me]
@@ -293,29 +404,29 @@
     def gu_copy(g, t):
         source = w_gate if t < 2 else w_up
         return pltpu.make_async_copy(
-            source.at[pl.ds(pl.multiple_of(chunk(g) * part, 128), part), (t % 2) * half : (t % 2 + 1) * half],
-            gu_tiles.at[t % 2],
-            gu_sem.at[t % 2],
+            source.at[pl.ds(at_column(g), part), (t % 2) * half : (t % 2 + 1) * half], gu_tiles.at[t], gu_sem.at[t]
         )
 
     def down_copy(g, t):
+        slot = lax.rem(g, 2)
         return pltpu.make_async_copy(
-            w_down.at[t * half : (t + 1) * half, pl.ds(pl.multiple_of(chunk(g) * part, 128), part)],
-            down_tiles.at[t],
-            down_sem.at[t],
+            w_down.at[t * half : (t + 1) * half, pl.ds(at_column(g), part)],
+            down_tiles.at[slot, t],
+            down_sem.at[slot, t],
         )
 
-    def in_copy(j, t, k):
-        start = chunk(j) * part + t * slab
+    def in_copy(j, k):
+        slot = lax.rem(j, 2)
         return pltpu.make_async_copy(
-            (w_gate, w_up)[k].at[pl.ds(pl.multiple_of(start, 128), slab), :],
-            in_tiles.at[t, k],
-            in_sem.at[t, k],
+            (w_gate, w_up)[k].at[pl.ds(at_column(j), part), :], in_tiles.at[slot, k], in_sem.at[slot, k]
         )
 
     def rs_x(q):
-        src = partial.at[q, pl.ds(pl.multiple_of((1 - x) * column, rows), column), :]
+        src = partial.at[q, pl.ds(pl.multiple_of((1 - x) * column, rows), column), 0:main]
         return remote(src, from_x.at[q], rx_send.at[q], rx_recv.at[q], beside)
+
+    def rs_edge(q):
+        return remote(edge_out.at[q], edge_in.at[q], ee_send.at[q], ee_recv.at[q], beside)
 
     def rs_up(q, first, count):
         return remote(
@@ -339,18 +450,28 @@
         ref = from_above.at[q, 0 : count * rows, :]
         remote(ref, ref, rz_send.at[q, 1], rd_recv.at[q], above).wait_recv()
 
+    spans = (slice(0, main), slice(main, part), slice(part, part + edge))
+
     def total(q, level, *more):
-        mine = partial[q, pl.ds(pl.multiple_of(x * column + level * rows, rows), rows), :].astype(F32)
-        mine += from_x[q, level * rows : (level + 1) * rows, :].astype(F32)
+        near = pl.ds(pl.multiple_of(x * column + level * rows, rows), rows)
+        other = pl.ds(pl.multiple_of((1 - x) * column + level * rows, rows), rows)
+        values = [
+            partial[q, near, 0:main].astype(F32) + from_x[q, level * rows : (level + 1) * rows, :].astype(F32),
+            partial[q, near, main:part].astype(F32),
+            partial[q, other, main:part].astype(F32),
+        ]
         for ref, at in more:
-            mine += ref[q, at * rows : (at + 1) * rows, :].astype(F32)
-        return mine.astype(BF16)
-
-    def put(q, at, value):
-        onward[q, at * rows : (at + 1) * rows, :] = value
-
-    def emit(q, value):
-        cols = pl.ds(pl.multiple_of(chunk(q) * part, 128), part)
+            values = [
+                value + ref[q, at * rows : (at + 1) * rows, span].astype(F32) for value, span in zip(values, spans)
+            ]
+        return values
+
+    def put(q, at, values):
+        for value, span in zip(values, spans):
+            onward[q, at * rows : (at + 1) * rows, span] = value.astype(BF16)
+
+    def store(q, first, value):
+        cols = pl.ds(pl.multiple_of(at_column(q) + first, 128), value.shape[1])
 
         @pl.when(q < steps)
         def _():
@@ -359,6 +480,11 @@
         @pl.when(q >= steps)
         def _():
             input_grad[:, cols] = value
+
+    def emit(q, values):
+        store(q, 0, values[0].astype(BF16))
+        edge_keep[q] = values[1]
+        edge_out[q] = values[2].astype(BF16)
 
     def stage_one(q):
         rs_x(q).wait_recv()
@@ -422,22 +548,30 @@
             below_arrived(q, 1)
             emit(q, total(q, 3, (from_below, 0)))
 
+        rs_edge(q).start()
+
+    def stage_five(q):
+        rs_edge(q).wait_recv()
+        store(q, main, (edge_keep[q] + edge_in[q].astype(F32)).astype(BF16))
+
     mine = pl.ds(pl.multiple_of((x * levels + z) * rows, rows), rows)
 
     def own_copy(g, source):
         return pltpu.make_async_copy(
-            source.at[:, pl.ds(pl.multiple_of(chunk(g) * part, 128), part)], blocks.at[g, mine, :], own_sem.at[g]
+            source.at[:, pl.ds(at_column(g), part)], blocks.at[g, mine, :], own_sem.at[g]
         )
 
     for s in range(steps):
         own_copy(s, tokens).start()
     for s in range(steps):
         own_copy(steps + s, cotangent).start()
+    for t in range(4):
+        gu_copy(0, t).start()
     for t in range(2):
-        gu_copy(0, t).start()
         down_copy(steps, t).start()
-        for k in range(2):
-            in_copy(0, t, k).start()
+        down_copy(steps + 1, t).start()
+        in_copy(0, t).start()
+        in_copy(1, t).start()
 
     barrier = pltpu.get_barrier_semaphore()
 
@@ -464,38 +598,35 @@
     def _():
         pl.semaphore_wait(barrier, 5)
 
-    for s in range(steps):
-        own_copy(s, tokens).wait()
-        own_copy(steps + s, cotangent).wait()
-
-    own(0)
-    own(1)
+    @pl.loop(0, ahead)
+    def _(i):
+        first_acts(i - ahead)
+        second_acts(i - ahead)
+        third_acts(i - ahead)
+
     gate[...] = jnp.zeros_like(gate)
     up[...] = jnp.zeros_like(up)
     back[...] = jnp.zeros_like(back)
-    for h in range(1, levels):
-        relay(0, h)
 
     @pl.loop(0, steps)
     def _(g):
-        own(g + 2)
-        relay(g + 1, 1)
+        first_acts(g)
         arrived(g)
         exchange(g)
         for t in range(4):
             gu_copy(g, t).wait()
             target, at = (gate, up)[t // 2], t % 2
             target[:, at * half : (at + 1) * half] += jnp.dot(
-                blocks[g], gu_tiles[at], preferred_element_type=F32
+                blocks[g], gu_tiles[t], preferred_element_type=F32
             )
-            if t < 2:
-                gu_copy(g, t + 2).start()
-            else:
-                @pl.when(g < steps - 1)
-                def _():
-                    gu_copy(g + 1, t - 2).start()
-            if t in (1, 3):
-                relay(g + 1, t // 2 + 2)
+
+            @pl.when(g < steps - 1)
+            def _():
+                gu_copy(g + 1, t).start()
+
+            if t == 1:
+                second_acts(g)
+        third_acts(g)
 
     lines = 32
 
@@ -510,43 +641,40 @@
 
     @pl.loop(steps, 2 * steps)
     def _(g):
-        @pl.when(g + 2 < 2 * steps)
-        def _():
-            own(g + 2)
-
-        @pl.when(g + 1 < 2 * steps)
-        def _():
-            relay(g + 1, 1)
-
+        first_acts(g)
         for t in range(2):
             down_copy(g, t).wait()
-        product = jnp.dot(hidden[:, :half], down_tiles[0], preferred_element_type=F32)
-        product += jnp.dot(hidden[:, half:], down_tiles[1], preferred_element_type=F32)
+        slot = lax.rem(g, 2)
+        product = jnp.dot(hidden[:, :half], down_tiles[slot, 0], preferred_element_type=F32)
+        product += jnp.dot(hidden[:, half:], down_tiles[slot, 1], preferred_element_type=F32)
         partial[g - steps] = product.astype(BF16)
-
-        @pl.when(g + 1 < 2 * steps)
-        def _():
-            relay(g + 1, 2)
-
+        second_acts(g)
         arrived(g)
         exchange(g)
         for t in range(2):
-            back[:, t * half : (t + 1) * half] += right_trans(blocks[g], down_tiles[t])
-
-            @pl.when(g + 1 < 2 * steps)
+            back[:, t * half : (t + 1) * half] += right_trans(blocks[g], down_tiles[slot, t])
+
+            @pl.when(g + 2 < 2 * steps)
             def _():
-                down_copy(g + 1, t).start()
-
-        @pl.when(g + 1 < 2 * steps)
-        def _():
-            relay(g + 1, 3)
-
-        @pl.when(g == 2 * steps - 2)
-        def _():
-            for j in range(steps - 1):
-                rs_x(j).start()
-
-    rs_x(steps - 1).start()
+                down_copy(g + 2, t).start()
+        third_acts(g)
+
+        @pl.when(g >= steps + 2)
+        def _():
+            rs_x(g - steps - 2).start()
+
+        @pl.when(g >= steps + 4)
+        def _():
+            stage_one(g - steps - 4)
+
+        @pl.when(g >= steps + 6)
+        def _():
+            stage_two(g - steps - 6)
+
+    @pl.loop(steps - 2, steps)
+    def _(j):
+        rs_x(j).start()
+
 
     @pl.loop(0, held // lines)
     def _(i):
@@ -559,50 +687,51 @@
     for k, source in ((1, dgate), (2, dup)):
         for copy in units_copies(source, k):
             copy.start()
-    units_arrived(0, across)
-    units_forward(0).start()
-
     last = 2 * steps
 
-    @pl.loop(0, last + 3)
+    def later(i, lag, stage):
+        @pl.when((i >= lag) & (i < last + lag))
+        def _():
+            stage(i - lag)
+
+    @pl.loop(0, last + 2)
     def _(i):
         @pl.when(i < steps)
         def _():
-            for t in range(2):
+            slot = lax.rem(i, 2)
+            for k in range(2):
+                in_copy(i, k).wait()
+            product = right_trans(dgate[...], in_tiles[slot, 0]) + right_trans(dup[...], in_tiles[slot, 1])
+            partial[i + steps] = product.astype(BF16)
+
+            @pl.when(i + 2 < steps)
+            def _():
                 for k in range(2):
-                    in_copy(i, t, k).wait()
-                product = right_trans(dgate[...], in_tiles[t, 0]) + right_trans(dup[...], in_tiles[t, 1])
-                partial[i + steps, :, t * slab : (t + 1) * slab] = product.astype(BF16)
-
-                @pl.when(i + 1 < steps)
-                def _():
-                    for k in range(2):
-                        in_copy(i + 1, t, k).start()
+                    in_copy(i + 2, k).start()
+
             rs_x(i + steps).start()
 
-        @pl.when(i < last)
-        def _():
-            stage_one(i)
-
-        @pl.when((i >= 1) & (i < last + 1))
-        def _():
-            stage_two(i - 1)
-
-        @pl.when((i >= 2) & (i < last + 2))
-        def _():
-            stage_three(i - 2)
-
-        @pl.when(i >= 3)
-        def _():
-            stage_four(i - 3)
-
-        @pl.when(i == last)
+        later(i, -4, stage_one)
+        later(i, -2, stage_two)
+        later(i, 0, stage_three)
+        later(i, 2, stage_four)
+
+        @pl.when(i == 2)
+        def _():
+            units_arrived(0, across)
+            units_forward(0).start()
+
+        @pl.when(i == last - 5)
         def _():
             units_arrived(1, across)
             units_forward(1).start()
 
-    units_arrived(2, across)
-    units_forward(2).start()
+        @pl.when(i == last - 1)
+        def _():
+            units_arrived(2, across)
+            units_forward(2).start()
+
+    pl.loop(0, last)(stage_five)
 
     @pl.loop(0, 2 * steps)
     def _(g):
@@ -610,15 +739,26 @@
             @pl.when((z < top) & (z >= h))
             def _():
                 go_up(g, h).wait_send()
+                rim_up(g, h).wait_send()
 
             @pl.when((z > 0) & (z + h <= top))
             def _():
                 go_down(g, h).wait_send()
-
-        for level in range(levels):
-            go_x(g, level).wait_send()
+                rim_down(g, h).wait_send()
+
+        for h in range(1, levels):
+            @pl.when(z >= h)
+            def _():
+                go_x(g, z - h).wait_send()
+
+            @pl.when(z + h <= top)
+            def _():
+                go_x(g, z + h).wait_send()
+
+        own_x(g).wait_send()
         exchange_done(g)
         rs_x(g).wait_send()
+        rs_edge(g).wait_send()
 
         @pl.when(z == 0)
         def _():
@@ -640,8 +780,15 @@
 
     for kind in range(2):
         for other in (twin, across, (1 - y) * CORES + (1 - core)):
-            ref = features.at[kind, other]
-            remote(ref, ref, ex_send.at[0], ex_recv.at[kind, other], (twin, place)).wait_recv()
+            for piece in range(HALVES):
+                for level in range(levels + 1):
+                    first, size = (x * levels + level) * rows, rows
+                    if level == levels:
+                        first, size = (1 - x) * column, column
+                    lines = pl.ds(pl.multiple_of(first, rows), size)
+                    ref = features.at[kind, other, lines, piece * part : (piece + 1) * part]
+                    recv = ex_recv.at[kind, other, piece, level]
+                    remote(ref, ref, ex_send.at[0, level], recv, (twin, place)).wait_recv()
     for k, source in enumerate((hidden, dgate, dup)):
         local, far, near = units_copies(source, k)
         local.wait()
@@ -657,7 +804,9 @@
     inner = w_gate.shape[1]
     held, part = rows * tp, width // dp
     levels = tp // COLS
-    half, slab = inner // 2, part // 2
+    half, sub, count = inner // 2, part // HALVES, HALVES * dp
+    edge = sub // 7 // 128 * 128
+    main = sub - edge
     hbm, vmem = pl.BlockSpec(memory_space=pl.ANY), pl.BlockSpec(memory_space=pltpu.VMEM)
     dma = pltpu.SemaphoreType.DMA
     chain = (levels - 1) * rows
@@ -672,27 +821,32 @@
             jax.ShapeDtypeStruct((3, dp, held, inner), BF16),
         ],
         scratch_shapes=[
-            pltpu.VMEM((2 * dp, held, part), BF16),
+            pltpu.VMEM((2 * count, held, sub), BF16),
             pltpu.VMEM((held, inner), F32),
             pltpu.VMEM((held, inner), F32),
             pltpu.VMEM((held, inner), F32),
             pltpu.VMEM((held, inner), BF16),
             pltpu.VMEM((held, inner), BF16),
             pltpu.VMEM((held, inner), BF16),
-            pltpu.VMEM((2 * dp, held, part), BF16),
-            pltpu.VMEM((2 * dp, levels * rows, part), BF16),
-            pltpu.VMEM((2 * dp, chain, part), BF16),
-            pltpu.VMEM((2 * dp, chain, part), BF16),
-            pltpu.VMEM((2 * dp, chain, part), BF16),
-            pltpu.VMEM((2, part, half), BF16),
-            pltpu.VMEM((2, half, part), BF16),
-            pltpu.VMEM((2, 2, slab, inner), BF16),
-            dma((2 * dp,)), dma((2,)), dma((2,)), dma((2, 2)),
-            dma((2 * dp, 3)), dma((2 * dp, 3)), dma((2 * dp, 3)), dma((2 * dp, 3)),
-            dma((2 * dp, levels)), dma((2 * dp, levels)),
-            dma((2 * dp,)), dma((2, dp)),
+            pltpu.VMEM((2 * count, held, sub), BF16),
+            pltpu.VMEM((2 * count, levels * rows, main), BF16),
+            pltpu.VMEM((2 * count, chain, sub + edge), BF16),
+            pltpu.VMEM((2 * count, chain, sub + edge), BF16),
+            pltpu.VMEM((2 * count, chain, sub + edge), BF16),
+            pltpu.VMEM((2 * count, rows, edge), BF16),
+            pltpu.VMEM((2 * count, rows, edge), BF16),
+            pltpu.VMEM((2 * count, rows, edge), F32),
+            pltpu.VMEM((4, sub, half), BF16),
+            pltpu.VMEM((2, 2, half, sub), BF16),
+            pltpu.VMEM((2, 2, sub, inner), BF16),
+            dma((2 * count,)), dma((4,)), dma((2, 2)), dma((2, 2)),
+            dma((2 * count, 3)), dma((2 * count, 3)), dma((2 * count, 3)), dma((2 * count, 3)),
+            dma((2 * count, levels)), dma((2 * count, levels)),
+            dma((2 * count, 3)), dma((2 * count, 3)), dma((2 * count, 3)), dma((2 * count, 3)),
+            dma((2 * count,)), dma((2 * count,)),
+            dma((2 * count, levels + 1)), dma((2, dp, HALVES, levels + 1)),
             dma((3, 3)), dma((3, dp)), dma((3,)),
-            dma((2 * dp,)), dma((2 * dp,)), dma((2 * dp, 2)), dma((2 * dp,)), dma((2 * dp,)),
+            dma((2 * count,)), dma((2 * count,)), dma((2 * count, 2)), dma((2 * count,)), dma((2 * count,)),
         ],
         compiler_params=pltpu.CompilerParams(
             collective_id=0, has_side_effects=True, vmem_limit_bytes=67_043_328
@@ -700,34 +854,82 @@
         name="fused",
     )(tokens, cotangent, w_gate, w_up, w_down)
 
-    def grad(left, at, right, of):
-        count = left.shape[-1]
-        cols = right.shape[-1]
-        tile = count // 2 if count % 256 == 0 else 128
-
-        def kernel(l_ref, r_ref, out):
-            out[...] = lax.dot_general(
-                l_ref[...].reshape(dp * held, tile),
-                r_ref[...].reshape(dp * held, cols),
+    tile = 256 if part % 256 == 0 and inner % 256 == 0 else 128
+    early, late = inner // tile, part // tile
+    depth = dp * held
+
+    def grads(hidden_ref, cot_ref, tok_ref, units_ref, mixed_ref, in_ref, down, gate, up, mixed_out, in_out, both, sem):
+        step = pl.program_id(0)
+
+        def fetch(k):
+            return pltpu.make_async_copy(units_ref.at[1 + k], both.at[k], sem.at[k])
+
+        def product(left, right):
+            return lax.dot_general(
+                left.reshape(depth, left.shape[-1]),
+                right.reshape(depth, right.shape[-1]),
                 (((0,), (0,)), ((), ())),
                 preferred_element_type=F32,
             )
 
-        return pl.pallas_call(
-            kernel,
-            grid=(count // tile,),
-            in_specs=[
-                pl.BlockSpec((None, dp, held, tile), lambda i: (at, 0, 0, i)),
-                pl.BlockSpec((None, dp, held, cols), lambda i: (of, 0, 0, 0)),
-            ],
-            out_specs=pl.BlockSpec((tile, cols), lambda i: (i, 0)),
-            out_shape=jax.ShapeDtypeStruct((count, cols), F32),
-            compiler_params=pltpu.CompilerParams(vmem_limit_bytes=60 << 20),
-        )(left, right)
-
-    gate_grad = grad(features, 0, units, 1)
-    up_grad = grad(features, 0, units, 2)
-    down_grad = grad(units, 0, features, 1)
+        @pl.when(step == 0)
+        def _():
+            for k in range(2):
+                fetch(k).start()
+            mixed_out[...] = mixed_ref[...]
+            in_out[...] = in_ref[...]
+
+        @pl.when(step < early)
+        def _():
+            down[...] = product(hidden_ref[...], cot_ref[...])
+
+        @pl.when(step == early)
+        def _():
+            for k in range(2):
+                fetch(k).wait()
+
+        @pl.when(step >= early)
+        def _():
+            gate[...] = product(tok_ref[...], both[0])
+            up[...] = product(tok_ref[...], both[1])
+
+    whole = pl.BlockSpec((rows, width), lambda i: (0, 0))
+
+    def first(i):
+        return jnp.minimum(i, early - 1)
+
+    def second(i):
+        return jnp.maximum(i - early, 0)
+
+    down_grad, gate_grad, up_grad, mixed, input_grad = pl.pallas_call(
+        grads,
+        grid=(early + late,),
+        in_specs=[
+            pl.BlockSpec((None, dp, held, tile), lambda i: (0, 0, 0, first(i))),
+            pl.BlockSpec((None, dp, held, part), lambda i: (1, 0, 0, 0)),
+            pl.BlockSpec((None, dp, held, tile), lambda i: (0, 0, 0, second(i))),
+            hbm,
+            whole,
+            whole,
+        ],
+        out_specs=[
+            pl.BlockSpec((tile, part), lambda i: (first(i), 0)),
+            pl.BlockSpec((tile, inner), lambda i: (second(i), 0)),
+            pl.BlockSpec((tile, inner), lambda i: (second(i), 0)),
+            whole,
+            whole,
+        ],
+        out_shape=[
+            jax.ShapeDtypeStruct((inner, part), F32),
+            jax.ShapeDtypeStruct((part, inner), F32),
+            jax.ShapeDtypeStruct((part, inner), F32),
+            jax.ShapeDtypeStruct((rows, width), BF16),
+            jax.ShapeDtypeStruct((rows, width), BF16),
+        ],
+        scratch_shapes=[pltpu.VMEM((2, dp, held, inner), BF16), dma((2,))],
+        compiler_params=pltpu.CompilerParams(vmem_limit_bytes=60 << 20),
+        name="grads",
+    )(units, features, features, units, mixed, input_grad)
     return mixed, input_grad, gate_grad, up_grad, down_grad
 
 

time: 226 us -> 200 us (0.88)
  Pallas kernels: 223 us -> 199 us
    pallas_call x1, Pallas kernels: 190 us -> 171 us  [fused_body(): pl.pallas_call(fused_kernel, in_specs=[hbm] * 5, out_specs=[vmem, vmem, h...]
    pallas_call x3 -> x1, Pallas kernels: 33.1 us -> 27.7 us  [fused_body(): pl.pallas_call(grads, grid=(early + late,), in_specs=[pl.BlockSpec((None,...]
where the time goes in v1:
time: 200 us; the launch traced here: 199 us
  Pallas kernels  199 us (100%)
    pallas_call x1, Pallas kernels, fused_body(): pl.pallas_call(fused_kernel, in_specs=[hbm] * 5, out_specs=[vmem, vmem, h...  171 us
    pallas_call x1, Pallas kernels, fused_body(): pl.pallas_call(grads, grid=(early + late,), in_specs=[pl.BlockSpec((None,...  27.7 us

profile of v1, /device:TPU:0, one launch (start us, length us, event | category | flops | bytes accessed | tf_op | source)
XLA Modules:
  0.0 199.3 jit_solution(10964953901928822550)
XLA Ops:
  0.6 171.0 %fused.1 = (bf16[32,7168]{1,0:T(8,128)(2,1)}, bf16[32,7168]{1,0:T(8,128)(2,1)}, bf16[2,4,256,1792]{3,2,1,0:T(8,128)(2,1)}, bf16[3,4,256,1536]{3,2,1,0:T(8,128)(2,1)}) custom-call(bf16[32,7168]{1,0:T(8,128)(2,1)} %tokens.1, bf16[32,7168]{1,0:T(8,128)(2,1)} %cotangent.1, bf16[7168,1536]{1,0:T(8,128)(2,1)} %w_gate.1, bf16[7168,1536]{1,0:T(8,128)(2,1)} %w_up.1, ...), custom_call_target="tpu_custom_call" | custom-call | tf_op jit(solution)/shard_map/fused/pallas_call | solution.py:813
  171.6 27.7 %grads.1 = (f32[1536,1792]{1,0:T(8,128)}, f32[1792,1536]{1,0:T(8,128)}, f32[1792,1536]{1,0:T(8,128)}, bf16[32,7168]{1,0:T(8,128)(2,1)}, bf16[32,7168]{1,0:T(8,128)(2,1)}) custom-call(bf16[3,4,256,1536]{3,2,1,0:T(8,128)(2,1)} %get-tuple-element.14.hidden_ref.units_ref, bf16[2,4,256,1792]{3,2,1,0:T(8,128)(2,1)} %get-tuple-element.15.cot_ref.tok_ref, ...), custom_call_target="tpu_custom_call" | custom-call | tf_op jit(solution)/shard_map/grads/pallas_call | solution.py:904

commit v2 on v1

--- a/solution.py
+++ b/solution.py
@@ -157,7 +157,7 @@
 
 
 MESH = pl.DeviceIdType.MESH
-CORES, COLS, HALVES = 2, 2, 2
+CORES, COLS, HALVES, GATHER_EDGES, AHEAD = 2, 2, 2, 1, 8
 
 
 def fused_kernel(
@@ -183,7 +183,8 @@
     half = inner // 2
     edge = part // 7 // 128 * 128
     main = part - edge
-    ahead = 8
+    bulk = part - GATHER_EDGES * edge
+    ahead = AHEAD
     top = levels - 1
     beside = (me, z * COLS + (1 - x))
     above, below = (me, place + COLS), (me, place - COLS)
@@ -207,31 +208,31 @@
         return blocks.at[g, pl.ds(pl.multiple_of((col * levels + level) * rows, rows), rows), first:last]
 
     def rim(g, col, level):
-        return spot(g, col, level, main, part)
+        return spot(g, col, level, bulk, part)
 
     def go_up(g, h):
         ref = spot(g, x, z - h)
-        return remote(ref, ref, up_send.at[g, h], up_recv.at[g, h], above)
+        return remote(ref, ref, up_send.at[h], up_recv.at[g, h], above)
 
     def go_down(g, h):
         ref = spot(g, x, z + h)
-        return remote(ref, ref, dn_send.at[g, h], dn_recv.at[g, h], below)
+        return remote(ref, ref, dn_send.at[h], dn_recv.at[g, h], below)
 
     def rim_up(g, h):
         ref = rim(g, 1 - x, z - h)
-        return remote(ref, ref, eu_send.at[g, h], eu_recv.at[g, h], above)
+        return remote(ref, ref, eu_send.at[h], eu_recv.at[g, h], above)
 
     def rim_down(g, h):
         ref = rim(g, 1 - x, z + h)
-        return remote(ref, ref, ed_send.at[g, h], ed_recv.at[g, h], below)
+        return remote(ref, ref, ed_send.at[h], ed_recv.at[g, h], below)
 
     def own_x(g):
         ref = spot(g, x, z)
-        return remote(ref, ref, x_send.at[g, z], x_recv.at[g, z], beside)
+        return remote(ref, ref, x_send.at[levels], x_recv.at[g, z], beside)
 
     def go_x(g, level):
-        ref = spot(g, x, level, 0, main)
-        return remote(ref, ref, x_send.at[g, level], x_recv.at[g, level], beside)
+        ref = spot(g, x, level, 0, bulk)
+        return remote(ref, ref, x_send.at[level], x_recv.at[g, level], beside)
 
     def own(g):
         @pl.when(g < steps)
@@ -255,7 +256,7 @@
 
     def turn(g):
         ref = spot(g, 1 - x, z)
-        remote(ref, ref, x_send.at[g, z], x_recv.at[g, z], beside).wait_recv()
+        remote(ref, ref, x_send.at[levels], x_recv.at[g, z], beside).wait_recv()
 
         @pl.when(z < top)
         def _():
@@ -269,7 +270,7 @@
         @pl.when(z >= h)
         def _():
             ref = spot(g, x, z - h)
-            remote(ref, ref, up_send.at[g, h - 1], up_recv.at[g, h - 1], below).wait_recv()
+            remote(ref, ref, up_send.at[h - 1], up_recv.at[g, h - 1], below).wait_recv()
             if h < top:
                 @pl.when(z < top)
                 def _():
@@ -281,7 +282,7 @@
         @pl.when(z + h <= top)
         def _():
             ref = spot(g, x, z + h)
-            remote(ref, ref, dn_send.at[g, h - 1], dn_recv.at[g, h - 1], above).wait_recv()
+            remote(ref, ref, dn_send.at[h - 1], dn_recv.at[g, h - 1], above).wait_recv()
             if h < top:
                 @pl.when(z > 0)
                 def _():
@@ -294,7 +295,7 @@
         @pl.when(z >= h)
         def _():
             ref = rim(g, 1 - x, z - h)
-            remote(ref, ref, eu_send.at[g, h - 1], eu_recv.at[g, h - 1], below).wait_recv()
+            remote(ref, ref, eu_send.at[h - 1], eu_recv.at[g, h - 1], below).wait_recv()
             if h < top:
                 @pl.when(z < top)
                 def _():
@@ -303,7 +304,7 @@
         @pl.when(z + h <= top)
         def _():
             ref = rim(g, 1 - x, z + h)
-            remote(ref, ref, ed_send.at[g, h - 1], ed_recv.at[g, h - 1], above).wait_recv()
+            remote(ref, ref, ed_send.at[h - 1], ed_recv.at[g, h - 1], above).wait_recv()
             if h < top:
                 @pl.when(z > 0)
                 def _():
@@ -332,26 +333,26 @@
         for h in range(1, levels):
             @pl.when(z >= h)
             def _():
-                ref = spot(g, 1 - x, z - h, 0, main)
-                remote(ref, ref, x_send.at[g, z - h], x_recv.at[g, z - h], beside).wait_recv()
+                ref = spot(g, 1 - x, z - h, 0, bulk)
+                remote(ref, ref, x_send.at[z - h], x_recv.at[g, z - h], beside).wait_recv()
 
             @pl.when(z + h <= top)
             def _():
-                ref = spot(g, 1 - x, z + h, 0, main)
-                remote(ref, ref, x_send.at[g, z + h], x_recv.at[g, z + h], beside).wait_recv()
+                ref = spot(g, 1 - x, z + h, 0, bulk)
+                remote(ref, ref, x_send.at[z + h], x_recv.at[g, z + h], beside).wait_recv()
 
     def shared(g, who):
         piece = lax.rem(g, HALVES)
         return features.at[g // steps, who, :, pl.ds(pl.multiple_of(piece * part, 128), part)]
 
     def local_share(g):
-        return pltpu.make_async_copy(blocks.at[g], shared(g, me), ex_send.at[g, 0])
+        return pltpu.make_async_copy(blocks.at[g], shared(g, me), ex_send.at[levels + 1])
 
     def lines_share(g, first, count, index):
         lines = pl.ds(pl.multiple_of(first, rows), count)
         recv = ex_recv.at[g // steps, me, lax.rem(g, HALVES), index]
         return remote(
-            blocks.at[g, lines, :], shared(g, me).at[lines, :], ex_send.at[g, index], recv, (owner(g), place)
+            blocks.at[g, lines, :], shared(g, me).at[lines, :], ex_send.at[index], recv, (owner(g), place)
         )
 
     def block_share(g, level):
@@ -373,17 +374,6 @@
         @pl.when(owner(g) != me)
         def _():
             rest_share(g).start()
-
-    def exchange_done(g):
-        @pl.when(owner(g) == me)
-        def _():
-            local_share(g).wait()
-
-        @pl.when(owner(g) != me)
-        def _():
-            for level in range(levels):
-                block_share(g, level).wait_send()
-            rest_share(g).wait_send()
 
     def units_copies(src, k):
         dst = units.at[k, me]
@@ -423,32 +413,32 @@
 
     def rs_x(q):
         src = partial.at[q, pl.ds(pl.multiple_of((1 - x) * column, rows), column), 0:main]
-        return remote(src, from_x.at[q], rx_send.at[q], rx_recv.at[q], beside)
+        return remote(src, from_x.at[q], rx_send.at[0], rx_recv.at[q], beside)
 
     def rs_edge(q):
-        return remote(edge_out.at[q], edge_in.at[q], ee_send.at[q], ee_recv.at[q], beside)
-
-    def rs_up(q, first, count):
+        return remote(edge_out.at[q], edge_in.at[q], ee_send.at[0], ee_recv.at[q], beside)
+
+    def slot(ref, q, at):
+        return ref.at[q, at * rows : (at + 1) * rows, :]
+
+    def rs_up(q, level):
+        at = level - 1
         return remote(
-            onward.at[q, first * rows : (first + count) * rows, :],
-            from_below.at[q, 0 : count * rows, :],
-            rz_send.at[q, 0], ru_recv.at[q], above,
+            slot(onward, q, at), slot(from_below, q, at), rz_send.at[at], ru_recv.at[q, at], above
         )
 
-    def rs_down(q, first, count):
+    def rs_down(q, level):
         return remote(
-            onward.at[q, first * rows : (first + count) * rows, :],
-            from_above.at[q, 0 : count * rows, :],
-            rz_send.at[q, 1], rd_recv.at[q], below,
+            slot(onward, q, level), slot(from_above, q, level), rz_send.at[level], rd_recv.at[q, level], below
         )
 
-    def below_arrived(q, count):
-        ref = from_below.at[q, 0 : count * rows, :]
-        remote(ref, ref, rz_send.at[q, 0], ru_recv.at[q], below).wait_recv()
-
-    def above_arrived(q, count):
-        ref = from_above.at[q, 0 : count * rows, :]
-        remote(ref, ref, rz_send.at[q, 1], rd_recv.at[q], above).wait_recv()
+    def below_arrived(q, level):
+        ref = slot(from_below, q, level - 1)
+        remote(ref, ref, rz_send.at[level - 1], ru_recv.at[q, level - 1], below).wait_recv()
+
+    def above_arrived(q, level):
+        ref = slot(from_above, q, level)
+        remote(ref, ref, rz_send.at[level], rd_recv.at[q, level], above).wait_recv()
 
     spans = (slice(0, main), slice(main, part), slice(part, part + edge))
 
@@ -486,73 +476,103 @@
         edge_keep[q] = values[1]
         edge_out[q] = values[2].astype(BF16)
 
+    def up_with(q, level, *more):
+        put(q, level - 1, total(q, level, *more))
+        rs_up(q, level).start()
+
+    def down_with(q, level, *more):
+        put(q, level, total(q, level, *more))
+        rs_down(q, level).start()
+
     def stage_one(q):
         rs_x(q).wait_recv()
 
         @pl.when(z == 0)
         def _():
-            for level in (1, 2, 3):
-                put(q, level - 1, total(q, level))
-            rs_up(q, 0, 3).start()
+            for level in (3, 2, 1):
+                up_with(q, level)
 
         @pl.when(z == 3)
         def _():
             for level in (0, 1, 2):
-                put(q, level, total(q, level))
-            rs_down(q, 0, 3).start()
+                down_with(q, level)
 
     def stage_two(q):
         @pl.when(z == 1)
         def _():
-            below_arrived(q, 3)
-            for level in (2, 3):
-                put(q, level - 2, total(q, level, (from_below, level - 1)))
-            rs_up(q, 0, 2).start()
+            for level in (3, 2):
+                below_arrived(q, level)
+                up_with(q, level, (from_below, level - 1))
 
         @pl.when(z == 2)
         def _():
-            above_arrived(q, 3)
             for level in (0, 1):
-                put(q, level, total(q, level, (from_above, level)))
-            rs_down(q, 0, 2).start()
+                above_arrived(q, level)
+                down_with(q, level, (from_above, level))
 
     def stage_three(q):
         @pl.when(z == 2)
         def _():
-            below_arrived(q, 2)
-            put(q, 2, total(q, 3, (from_below, 1)))
-            rs_up(q, 2, 1).start()
+            below_arrived(q, 3)
+            up_with(q, 3, (from_below, 2))
 
         @pl.when(z == 1)
         def _():
-            above_arrived(q, 2)
-            put(q, 2, total(q, 0, (from_above, 0)))
-            rs_down(q, 2, 1).start()
+            above_arrived(q, 0)
+            down_with(q, 0, (from_above, 0))
 
     def stage_four(q):
         @pl.when(z == 0)
         def _():
+            above_arrived(q, 0)
+            emit(q, total(q, 0, (from_above, 0)))
+
+        @pl.when(z == 1)
+        def _():
+            below_arrived(q, 1)
             above_arrived(q, 1)
-            emit(q, total(q, 0, (from_above, 0)))
-
-        @pl.when(z == 1)
-        def _():
             emit(q, total(q, 1, (from_below, 0), (from_above, 1)))
 
         @pl.when(z == 2)
         def _():
-            emit(q, total(q, 2, (from_below, 0), (from_above, 2)))
+            below_arrived(q, 2)
+            above_arrived(q, 2)
+            emit(q, total(q, 2, (from_below, 1), (from_above, 2)))
 
         @pl.when(z == 3)
         def _():
-            below_arrived(q, 1)
-            emit(q, total(q, 3, (from_below, 0)))
+            below_arrived(q, 3)
+            emit(q, total(q, 3, (from_below, 2)))
 
         rs_edge(q).start()
 
     def stage_five(q):
         rs_edge(q).wait_recv()
         store(q, main, (edge_keep[q] + edge_in[q].astype(F32)).astype(BF16))
+
+    def sent(ref, sem):
+        remote(ref, ref, sem, rx_recv.at[0], beside).wait_send()
+
+    def lines_of(col, level, first=0, last=None):
+        start = pl.multiple_of((col * levels + level) * rows, rows)
+        return blocks.at[:, pl.ds(start, rows), first : part if last is None else last]
+
+    barrier = pltpu.get_barrier_semaphore()
+
+    def greet(device):
+        pl.semaphore_signal(barrier, inc=1, device_id=device, device_id_type=MESH)
+
+    greet(beside)
+    for other in (twin, across, (1 - y) * CORES + (1 - core)):
+        greet((other, place))
+
+    @pl.when(z < top)
+    def _():
+        greet(above)
+
+    @pl.when(z > 0)
+    def _():
+        greet(below)
 
     mine = pl.ds(pl.multiple_of((x * levels + z) * rows, rows), rows)
 
@@ -572,23 +592,6 @@
         down_copy(steps + 1, t).start()
         in_copy(0, t).start()
         in_copy(1, t).start()
-
-    barrier = pltpu.get_barrier_semaphore()
-
-    def greet(device):
-        pl.semaphore_signal(barrier, inc=1, device_id=device, device_id_type=MESH)
-
-    greet(beside)
-    for other in (twin, across, (1 - y) * CORES + (1 - core)):
-        greet((other, place))
-
-    @pl.when(z < top)
-    def _():
-        greet(above)
-
-    @pl.when(z > 0)
-    def _():
-        greet(below)
 
     @pl.when((z > 0) & (z < top))
     def _():
@@ -733,50 +736,40 @@
 
     pl.loop(0, last)(stage_five)
 
-    @pl.loop(0, 2 * steps)
-    def _(g):
-        for h in range(top):
-            @pl.when((z < top) & (z >= h))
-            def _():
-                go_up(g, h).wait_send()
-                rim_up(g, h).wait_send()
-
-            @pl.when((z > 0) & (z + h <= top))
-            def _():
-                go_down(g, h).wait_send()
-                rim_down(g, h).wait_send()
-
-        for h in range(1, levels):
-            @pl.when(z >= h)
-            def _():
-                go_x(g, z - h).wait_send()
-
-            @pl.when(z + h <= top)
-            def _():
-                go_x(g, z + h).wait_send()
-
-        own_x(g).wait_send()
-        exchange_done(g)
-        rs_x(g).wait_send()
-        rs_edge(g).wait_send()
-
-        @pl.when(z == 0)
-        def _():
-            rs_up(g, 0, 3).wait_send()
-
-        @pl.when(z == 1)
-        def _():
-            rs_up(g, 0, 2).wait_send()
-            rs_down(g, 2, 1).wait_send()
-
-        @pl.when(z == 2)
-        def _():
-            rs_up(g, 2, 1).wait_send()
-            rs_down(g, 0, 2).wait_send()
-
-        @pl.when(z == 3)
-        def _():
-            rs_down(g, 0, 3).wait_send()
+    for h in range(top):
+        @pl.when((z < top) & (z >= h))
+        def _():
+            sent(lines_of(x, z - h), up_send.at[h])
+            sent(lines_of(1 - x, z - h, bulk), eu_send.at[h])
+
+        @pl.when((z > 0) & (z + h <= top))
+        def _():
+            sent(lines_of(x, z + h), dn_send.at[h])
+            sent(lines_of(1 - x, z + h, bulk), ed_send.at[h])
+
+    for h in range(1, levels):
+        @pl.when(z >= h)
+        def _():
+            sent(lines_of(x, z - h, 0, bulk), x_send.at[z - h])
+
+        @pl.when(z + h <= top)
+        def _():
+            sent(lines_of(x, z + h, 0, bulk), x_send.at[z + h])
+
+    sent(lines_of(x, z), x_send.at[levels])
+    parts = steps // HALVES
+    remotes, locals_ = 2 * steps // parts * (parts - 1), 2 * steps // parts
+    for level in range(levels):
+        start = pl.multiple_of((x * levels + level) * rows, rows)
+        sent(blocks.at[0:remotes, pl.ds(start, rows), :], ex_send.at[level])
+    start = pl.multiple_of((1 - x) * column, rows)
+    sent(blocks.at[0:remotes, pl.ds(start, column), :], ex_send.at[levels])
+    same = blocks.at[0:locals_]
+    pltpu.make_async_copy(same, same, ex_send.at[levels + 1]).wait()
+    sent(partial.at[:, pl.ds(start, column), 0:main], rx_send.at[0])
+    for at in range(top):
+        sent(onward.at[:, at * rows : (at + 1) * rows, :], rz_send.at[at])
+    sent(edge_out, ee_send.at[0])
 
     for kind in range(2):
         for other in (twin, across, (1 - y) * CORES + (1 - core)):
@@ -788,7 +781,7 @@
                     lines = pl.ds(pl.multiple_of(first, rows), size)
                     ref = features.at[kind, other, lines, piece * part : (piece + 1) * part]
                     recv = ex_recv.at[kind, other, piece, level]
-                    remote(ref, ref, ex_send.at[0, level], recv, (twin, place)).wait_recv()
+                    remote(ref, ref, ex_send.at[level], recv, (twin, place)).wait_recv()
     for k, source in enumerate((hidden, dgate, dup)):
         local, far, near = units_copies(source, k)
         local.wait()
@@ -840,13 +833,13 @@
             pltpu.VMEM((2, 2, half, sub), BF16),
             pltpu.VMEM((2, 2, sub, inner), BF16),
             dma((2 * count,)), dma((4,)), dma((2, 2)), dma((2, 2)),
-            dma((2 * count, 3)), dma((2 * count, 3)), dma((2 * count, 3)), dma((2 * count, 3)),
-            dma((2 * count, levels)), dma((2 * count, levels)),
-            dma((2 * count, 3)), dma((2 * count, 3)), dma((2 * count, 3)), dma((2 * count, 3)),
-            dma((2 * count,)), dma((2 * count,)),
-            dma((2 * count, levels + 1)), dma((2, dp, HALVES, levels + 1)),
+            dma((3,)), dma((2 * count, 3)), dma((3,)), dma((2 * count, 3)),
+            dma((levels + 1,)), dma((2 * count, levels)),
+            dma((3,)), dma((2 * count, 3)), dma((3,)), dma((2 * count, 3)),
+            dma((1,)), dma((2 * count,)),
+            dma((levels + 2,)), dma((2, dp, HALVES, levels + 1)),
             dma((3, 3)), dma((3, dp)), dma((3,)),
-            dma((2 * count,)), dma((2 * count,)), dma((2 * count, 2)), dma((2 * count,)), dma((2 * count,)),
+            dma((1,)), dma((2 * count,)), dma((3,)), dma((2 * count, 3)), dma((2 * count, 3)),
         ],
         compiler_params=pltpu.CompilerParams(
             collective_id=0, has_side_effects=True, vmem_limit_bytes=67_043_328
@@ -854,8 +847,9 @@
         name="fused",
     )(tokens, cotangent, w_gate, w_up, w_down)
 
-    tile = 256 if part % 256 == 0 and inner % 256 == 0 else 128
-    early, late = inner // tile, part // tile
+    tall = 512 if inner % 512 == 0 else 128
+    tile = 256 if part % 256 == 0 else 128
+    early, late = inner // tall, part // tile
     depth = dp * held
 
     def grads(hidden_ref, cot_ref, tok_ref, units_ref, mixed_ref, in_ref, down, gate, up, mixed_out, in_out, both, sem):
@@ -905,7 +899,7 @@
         grads,
         grid=(early + late,),
         in_specs=[
-            pl.BlockSpec((None, dp, held, tile), lambda i: (0, 0, 0, first(i))),
+            pl.BlockSpec((None, dp, held, tall), lambda i: (0, 0, 0, first(i))),
             pl.BlockSpec((None, dp, held, part), lambda i: (1, 0, 0, 0)),
             pl.BlockSpec((None, dp, held, tile), lambda i: (0, 0, 0, second(i))),
             hbm,
@@ -913,7 +907,7 @@
             whole,
         ],
         out_specs=[
-            pl.BlockSpec((tile, part), lambda i: (first(i), 0)),
+            pl.BlockSpec((tall, part), lambda i: (first(i), 0)),
             pl.BlockSpec((tile, inner), lambda i: (second(i), 0)),
             pl.BlockSpec((tile, inner), lambda i: (second(i), 0)),
             whole,
@@ -927,7 +921,7 @@
             jax.ShapeDtypeStruct((rows, width), BF16),
         ],
         scratch_shapes=[pltpu.VMEM((2, dp, held, inner), BF16), dma((2,))],
-        compiler_params=pltpu.CompilerParams(vmem_limit_bytes=60 << 20),
+        compiler_params=pltpu.CompilerParams(vmem_limit_bytes=67_043_328),
         name="grads",
     )(units, features, features, units, mixed, input_grad)
     return mixed, input_grad, gate_grad, up_grad, down_grad

time: 200 us -> 192 us (0.960)
  Pallas kernels: 199 us -> 191 us
    pallas_call x1, Pallas kernels: 171 us -> 165 us  [fused_body(): pl.pallas_call(fused_kernel, in_specs=[hbm] * 5, out_specs=[vmem, vmem, h...]
where the time goes in v2:
time: 192 us
  Pallas kernels  191 us (99%)
    pallas_call x1, Pallas kernels, fused_body(): pl.pallas_call(fused_kernel, in_specs=[hbm] * 5, out_specs=[vmem, vmem, h...  165 us
    pallas_call x1, Pallas kernels, fused_body(): pl.pallas_call(grads, grid=(early + late,), in_specs=[pl.BlockSpec((None,...  25.7 us

profile of v2, /device:TPU:0, one launch (start us, length us, event | category | flops | bytes accessed | tf_op | source)
XLA Modules:
  0.0 191.5 jit_solution(3769181397900537162)
XLA Ops:
  0.6 165.1 %fused.1 = (bf16[32,7168]{1,0:T(8,128)(2,1)}, bf16[32,7168]{1,0:T(8,128)(2,1)}, bf16[2,4,256,1792]{3,2,1,0:T(8,128)(2,1)}, bf16[3,4,256,1536]{3,2,1,0:T(8,128)(2,1)}) custom-call(bf16[32,7168]{1,0:T(8,128)(2,1)} %tokens.1, bf16[32,7168]{1,0:T(8,128)(2,1)} %cotangent.1, bf16[7168,1536]{1,0:T(8,128)(2,1)} %w_gate.1, bf16[7168,1536]{1,0:T(8,128)(2,1)} %w_up.1, ...), custom_call_target="tpu_custom_call" | custom-call | tf_op jit(solution)/shard_map/fused/pallas_call | solution.py:806
  165.8 25.7 %grads.1 = (f32[1536,1792]{1,0:T(8,128)}, f32[1792,1536]{1,0:T(8,128)}, f32[1792,1536]{1,0:T(8,128)}, bf16[32,7168]{1,0:T(8,128)(2,1)}, bf16[32,7168]{1,0:T(8,128)(2,1)}) custom-call(bf16[3,4,256,1536]{3,2,1,0:T(8,128)(2,1)} %get-tuple-element.14.hidden_ref.units_ref, bf16[2,4,256,1792]{3,2,1,0:T(8,128)(2,1)} %get-tuple-element.15.cot_ref.tok_ref, ...), custom_call_target="tpu_custom_call" | custom-call | tf_op jit(solution)/shard_map/grads/pallas_call | solution.py:898
